TPU v7x, 8 devices: a whole 2x2x1 slice. The times are simulated.
8 devices in a mesh: dp: 1 (over z), sp: 8 (over y, x, core).
Axes of the slice: x: 2, y: 2, z: 1, core: 2. Of those that a mesh axis runs over, the one named last changes fastest.
Arguments:
- z_points: bfloat16 [4096, 128], P(('dp', 'sp'))
- x_points: bfloat16 [65536, 128], P(('dp', 'sp'))
- rhs_vals: bfloat16 [65536, 16], P(('dp', 'sp'))
- block_mask: int32 [8, 8], P(('dp', 'sp'))
- length_scale: float32 [1], replicated
- out_scale: float32 [1], replicated
Outputs:
- output: float32 [4096, 16], P(('dp', 'sp'))
All inputs are finite; a program needn't handle non-finite values.
Results may differ from a plain program's by a relative error of at most 0.001.
Values are sent between devices in bfloat16 or wider.
A program may use at most 1 GiB of HBM per device.

v0:
```python
import jax
import jax.numpy as jnp
from jax import lax
from jax.sharding import PartitionSpec as P


def block_product(z_rows, z_norm, x_rows, v_rows, ell_sq, scale_val):
    x_norm = jnp.einsum("nd,nd->n", x_rows, x_rows, preferred_element_type=jnp.float32)
    gram_blk = jnp.einsum("md,nd->mn", z_rows, x_rows, preferred_element_type=jnp.float32)
    sq_dist = jnp.maximum(z_norm[:, None] + x_norm[None, :] - 2.0 * gram_blk, 0.0)
    kern_blk = (scale_val * jnp.exp(-sq_dist / (2.0 * ell_sq))).astype(jnp.bfloat16)
    return jnp.dot(kern_blk, v_rows, preferred_element_type=jnp.float32)


def solution(mesh):
    group_size = mesh.shape["sp"]
    shift_pairs = [(dev_idx, (dev_idx + 1) % group_size) for dev_idx in range(group_size)]
    row_spec = P(("dp", "sp"), None)

    def local_fn(z_rows, x_rows, v_rows, mask_row, length_scale, out_scale):
        my_index = lax.axis_index("sp")
        ell_sq = length_scale[0] * length_scale[0]
        scale_val = out_scale[0]
        weights = mask_row[0].astype(jnp.float32)
        z_norm = jnp.einsum("md,md->m", z_rows, z_rows, preferred_element_type=jnp.float32)
        first_y = block_product(z_rows, z_norm, x_rows, v_rows, ell_sq, scale_val) * weights[my_index]

        def shift_step(step_idx, loop_state):
            x_cur, v_cur, y_acc = loop_state
            x_cur = lax.ppermute(x_cur, "sp", shift_pairs)
            v_cur = lax.ppermute(v_cur, "sp", shift_pairs)
            src_block = (my_index - step_idx) % group_size
            part_y = block_product(z_rows, z_norm, x_cur, v_cur, ell_sq, scale_val)
            return (x_cur, v_cur, y_acc + part_y * weights[src_block])

        final_state = lax.fori_loop(1, group_size, shift_step, (x_rows, v_rows, first_y))
        return final_state[2]

    return jax.shard_map(local_fn, mesh=mesh, in_specs=(row_spec, row_spec, row_spec, row_spec, P(None), P(None)), out_specs=row_spec, check_vma=False)
```

profile of v0, /device:TPU:0, one launch (start us, length us, event | category | flops | bytes accessed | tf_op | source)
XLA Modules:
  0.0 297.0 jit_solution(6654704174048396828)
XLA Ops:
  1.0 3.1 %copy.35 = bf16[8192,128]{1,0:T(8,128)(2,1)} copy(bf16[8192,128]{1,0:T(8,128)(2,1)} %param.9) | data formatting | bytes 4194304
  6.1 2.7 fusion.6
  8.9 8.8 %fusion.8 = f32[512,16]{0,1:T(8,128)S(1)} fusion(bf16[8192,16]{0,1:T(8,128)(2,1)S(1)} %copy.36, bf16[512,128]{1,0:T(8,128)(2,1)S(1)} %copy-done, bf16[8192,128]{1,0:T(8,128)(2,1)} %copy.35, f32[]{:T(128)} %bitcast.2, f32[8192]{0:T(1024)S(1)} %fusion.6, f32[512]{0:T(512)S(1)} %fusion.9, f32[]{:T(128)} %bitcast.20, f32[]{:T(128)} %bitcast.3), kind=kOutput, calls=%fused_computation.12 | convolution fusion | flops 1241522176 | bytes 2557964 | tf_op jit(solution)/shard_map/dot_general | solution.py:12
  17.7 278.7 %while.19 = (s32[]{:T(128)}, bf16[8192,128]{1,0:T(8,128)(2,1)}, bf16[8192,16]{0,1:T(8,128)(2,1)S(1)}, f32[512,16]{0,1:T(8,128)S(1)}, f32[]{:T(128)}, /*index=5*/...) while((s32[]{:T(128)}, bf16[8192,128]{1,0:T(8,128)(2,1)}, ...), condition=%wide.region_1.2_spmd, body=%wide.region_0.1_spmd.sunk | while | flops 1244667904 | bytes 18876808 | solution.py:36
  18.6 2.6 collective-permute-start.1
  21.8 26.2 %collective-permute-done.1 = bf16[8192,16]{0,1:T(8,128)(2,1)S(1)} collective-permute-done((bf16[8192,16]{0,1:T(8,128)(2,1)S(1)}, bf16[8192,16]{0,1:T(8,128)(2,1)S(1)}, u32[]{:S(2)}, u32[]{:S(2)}) %collective-permute-start.1) | collective-permute-done | bytes 262176 | tf_op jit(solution)/shard_map/while/body/eval_jaxpr/ppermute | solution.py:31
  50.6 7.9 %fusion.27 = f32[512,16]{0,1:T(8,128)S(1)} fusion(f32[512,16]{0,1:T(8,128)S(1)} %get-tuple-element.351, bf16[8192,16]{0,1:T(8,128)(2,1)S(1)} %collective-permute-done.1, bf16[512,128]{1,0:T(8,128)(2,1)S(1)} %get-tuple-element.368, bf16[8192,128]{1,0:T(8,128)(2,1)S(1)} %collective-permute-done, f32[]{:T(128)} %get-tuple-element.369, ...), kind=kOutput, calls=%fused_computation.5.clone.1 | convolution fusion | flops 1241530368 | bytes 2590732 | tf_op jit(solution)/shard_map/while/body/eval_jaxpr/dot_general | solution.py:12
  58.5 1.4 collective-permute-start.1
  60.6 27.1 %collective-permute-done.1 = bf16[8192,16]{0,1:T(8,128)(2,1)S(1)} collective-permute-done((bf16[8192,16]{0,1:T(8,128)(2,1)S(1)}, bf16[8192,16]{0,1:T(8,128)(2,1)S(1)}, u32[]{:S(2)}, u32[]{:S(2)}) %collective-permute-start.1) | collective-permute-done | bytes 262176 | tf_op jit(solution)/shard_map/while/body/eval_jaxpr/ppermute | solution.py:31
  88.9 1.4 copy.28
  90.2 7.9 %fusion.27 = f32[512,16]{0,1:T(8,128)S(1)} fusion(f32[512,16]{0,1:T(8,128)S(1)} %get-tuple-element.351, bf16[8192,16]{0,1:T(8,128)(2,1)S(1)} %collective-permute-done.1, bf16[512,128]{1,0:T(8,128)(2,1)S(1)} %get-tuple-element.368, bf16[8192,128]{1,0:T(8,128)(2,1)S(1)} %collective-permute-done, f32[]{:T(128)} %get-tuple-element.369, ...), kind=kOutput, calls=%fused_computation.5.clone.1 | convolution fusion | flops 1241530368 | bytes 2590732 | tf_op jit(solution)/shard_map/while/body/eval_jaxpr/dot_general | solution.py:12
  99.3 28.1 %collective-permute-done.1 = bf16[8192,16]{0,1:T(8,128)(2,1)S(1)} collective-permute-done((bf16[8192,16]{0,1:T(8,128)(2,1)S(1)}, bf16[8192,16]{0,1:T(8,128)(2,1)S(1)}, u32[]{:S(2)}, u32[]{:S(2)}) %collective-permute-start.1) | collective-permute-done | bytes 262176 | tf_op jit(solution)/shard_map/while/body/eval_jaxpr/ppermute | solution.py:31
  129.9 7.9 %fusion.27 = f32[512,16]{0,1:T(8,128)S(1)} fusion(f32[512,16]{0,1:T(8,128)S(1)} %get-tuple-element.351, bf16[8192,16]{0,1:T(8,128)(2,1)S(1)} %collective-permute-done.1, bf16[512,128]{1,0:T(8,128)(2,1)S(1)} %get-tuple-element.368, bf16[8192,128]{1,0:T(8,128)(2,1)S(1)} %collective-permute-done, f32[]{:T(128)} %get-tuple-element.369, ...), kind=kOutput, calls=%fused_computation.5.clone.1 | convolution fusion | flops 1241530368 | bytes 2590732 | tf_op jit(solution)/shard_map/while/body/eval_jaxpr/dot_general | solution.py:12
  138.5 28.5 %collective-permute-done.1 = bf16[8192,16]{0,1:T(8,128)(2,1)S(1)} collective-permute-done((bf16[8192,16]{0,1:T(8,128)(2,1)S(1)}, bf16[8192,16]{0,1:T(8,128)(2,1)S(1)}, u32[]{:S(2)}, u32[]{:S(2)}) %collective-permute-start.1) | collective-permute-done | bytes 262176 | tf_op jit(solution)/shard_map/while/body/eval_jaxpr/ppermute | solution.py:31
  169.5 7.9 %fusion.27 = f32[512,16]{0,1:T(8,128)S(1)} fusion(f32[512,16]{0,1:T(8,128)S(1)} %get-tuple-element.351, bf16[8192,16]{0,1:T(8,128)(2,1)S(1)} %collective-permute-done.1, bf16[512,128]{1,0:T(8,128)(2,1)S(1)} %get-tuple-element.368, bf16[8192,128]{1,0:T(8,128)(2,1)S(1)} %collective-permute-done, f32[]{:T(128)} %get-tuple-element.369, ...), kind=kOutput, calls=%fused_computation.5.clone.1 | convolution fusion | flops 1241530368 | bytes 2590732 | tf_op jit(solution)/shard_map/while/body/eval_jaxpr/dot_general | solution.py:12
  178.1 28.5 %collective-permute-done.1 = bf16[8192,16]{0,1:T(8,128)(2,1)S(1)} collective-permute-done((bf16[8192,16]{0,1:T(8,128)(2,1)S(1)}, bf16[8192,16]{0,1:T(8,128)(2,1)S(1)}, u32[]{:S(2)}, u32[]{:S(2)}) %collective-permute-start.1) | collective-permute-done | bytes 262176 | tf_op jit(solution)/shard_map/while/body/eval_jaxpr/ppermute | solution.py:31
  207.8 1.4 copy.28
  209.2 7.9 %fusion.27 = f32[512,16]{0,1:T(8,128)S(1)} fusion(f32[512,16]{0,1:T(8,128)S(1)} %get-tuple-element.351, bf16[8192,16]{0,1:T(8,128)(2,1)S(1)} %collective-permute-done.1, bf16[512,128]{1,0:T(8,128)(2,1)S(1)} %get-tuple-element.368, bf16[8192,128]{1,0:T(8,128)(2,1)S(1)} %collective-permute-done, f32[]{:T(128)} %get-tuple-element.369, ...), kind=kOutput, calls=%fused_computation.5.clone.1 | convolution fusion | flops 1241530368 | bytes 2590732 | tf_op jit(solution)/shard_map/while/body/eval_jaxpr/dot_general | solution.py:12
  217.8 28.5 %collective-permute-done.1 = bf16[8192,16]{0,1:T(8,128)(2,1)S(1)} collective-permute-done((bf16[8192,16]{0,1:T(8,128)(2,1)S(1)}, bf16[8192,16]{0,1:T(8,128)(2,1)S(1)}, u32[]{:S(2)}, u32[]{:S(2)}) %collective-permute-start.1) | collective-permute-done | bytes 262176 | tf_op jit(solution)/shard_map/while/body/eval_jaxpr/ppermute | solution.py:31
  247.5 1.4 copy.28
  248.8 7.9 %fusion.27 = f32[512,16]{0,1:T(8,128)S(1)} fusion(f32[512,16]{0,1:T(8,128)S(1)} %get-tuple-element.351, bf16[8192,16]{0,1:T(8,128)(2,1)S(1)} %collective-permute-done.1, bf16[512,128]{1,0:T(8,128)(2,1)S(1)} %get-tuple-element.368, bf16[8192,128]{1,0:T(8,128)(2,1)S(1)} %collective-permute-done, f32[]{:T(128)} %get-tuple-element.369, ...), kind=kOutput, calls=%fused_computation.5.clone.1 | convolution fusion | flops 1241530368 | bytes 2590732 | tf_op jit(solution)/shard_map/while/body/eval_jaxpr/dot_general | solution.py:12
  257.4 28.5 %collective-permute-done.1 = bf16[8192,16]{0,1:T(8,128)(2,1)S(1)} collective-permute-done((bf16[8192,16]{0,1:T(8,128)(2,1)S(1)}, bf16[8192,16]{0,1:T(8,128)(2,1)S(1)}, u32[]{:S(2)}, u32[]{:S(2)}) %collective-permute-start.1) | collective-permute-done | bytes 262176 | tf_op jit(solution)/shard_map/while/body/eval_jaxpr/ppermute | solution.py:31
  287.1 1.4 copy.28
  288.5 7.9 %fusion.27 = f32[512,16]{0,1:T(8,128)S(1)} fusion(f32[512,16]{0,1:T(8,128)S(1)} %get-tuple-element.351, bf16[8192,16]{0,1:T(8,128)(2,1)S(1)} %collective-permute-done.1, bf16[512,128]{1,0:T(8,128)(2,1)S(1)} %get-tuple-element.368, bf16[8192,128]{1,0:T(8,128)(2,1)S(1)} %collective-permute-done, f32[]{:T(128)} %get-tuple-element.369, ...), kind=kOutput, calls=%fused_computation.5.clone.1 | convolution fusion | flops 1241530368 | bytes 2590732 | tf_op jit(solution)/shard_map/while/body/eval_jaxpr/dot_general | solution.py:12
  (53 shorter events, 20.3 us)
Async XLA Ops:
  1.0 4.4 %copy-start.1 = (s32[1,8]{1,0:T(1,128)S(1)}, s32[1,8]{1,0:T(1,128)}, u32[]{:S(2)}) copy-start(s32[1,8]{1,0:T(1,128)} %param.11) | copy-start | bytes 100
  1.0 5.0 %copy-start = (bf16[512,128]{1,0:T(8,128)(2,1)S(1)}, bf16[512,128]{1,0:T(8,128)(2,1)}, u32[]{:S(2)}) copy-start(bf16[512,128]{1,0:T(8,128)(2,1)} %param.8) | copy-start | bytes 393220
  17.8 30.3 %collective-permute-start = (bf16[8192,128]{1,0:T(8,128)(2,1)}, bf16[8192,128]{1,0:T(8,128)(2,1)S(1)}, u32[]{:S(2)}, u32[]{:S(2)}) collective-permute-start(bf16[8192,128]{1,0:T(8,128)(2,1)} %get-tuple-element.349), channel_id=1, source_target_pairs={{0,1},{1,2},{2,3},{3,4},{4,5},{5,6},{6,7},{7,0}} | collective-permute-start | bytes 6291464 | tf_op jit(solution)/shard_map/while/body/eval_jaxpr/ppermute | solution.py:30
  18.6 29.4 %collective-permute-start.1 = (bf16[8192,16]{0,1:T(8,128)(2,1)S(1)}, bf16[8192,16]{0,1:T(8,128)(2,1)S(1)}, u32[]{:S(2)}, u32[]{:S(2)}) collective-permute-start(bf16[8192,16]{0,1:T(8,128)(2,1)S(1)} %get-tuple-element.350), channel_id=1, source_target_pairs={{0,1},{1,2},{2,3},{3,4},{4,5},{5,6},{6,7},{7,0}} | collective-permute-start | bytes 786440 | tf_op jit(solution)/shard_map/while/body/eval_jaxpr/ppermute | solution.py:31
  58.5 29.2 %collective-permute-start = (bf16[8192,128]{1,0:T(8,128)(2,1)}, bf16[8192,128]{1,0:T(8,128)(2,1)S(1)}, u32[]{:S(2)}, u32[]{:S(2)}) collective-permute-start(bf16[8192,128]{1,0:T(8,128)(2,1)} %get-tuple-element.349), channel_id=1, source_target_pairs={{0,1},{1,2},{2,3},{3,4},{4,5},{5,6},{6,7},{7,0}} | collective-permute-start | bytes 6291464 | tf_op jit(solution)/shard_map/while/body/eval_jaxpr/ppermute | solution.py:30
  58.5 29.2 %collective-permute-start.1 = (bf16[8192,16]{0,1:T(8,128)(2,1)S(1)}, bf16[8192,16]{0,1:T(8,128)(2,1)S(1)}, u32[]{:S(2)}, u32[]{:S(2)}) collective-permute-start(bf16[8192,16]{0,1:T(8,128)(2,1)S(1)} %get-tuple-element.350), channel_id=1, source_target_pairs={{0,1},{1,2},{2,3},{3,4},{4,5},{5,6},{6,7},{7,0}} | collective-permute-start | bytes 786440 | tf_op jit(solution)/shard_map/while/body/eval_jaxpr/ppermute | solution.py:31
  98.2 29.2 %collective-permute-start = (bf16[8192,128]{1,0:T(8,128)(2,1)}, bf16[8192,128]{1,0:T(8,128)(2,1)S(1)}, u32[]{:S(2)}, u32[]{:S(2)}) collective-permute-start(bf16[8192,128]{1,0:T(8,128)(2,1)} %get-tuple-element.349), channel_id=1, source_target_pairs={{0,1},{1,2},{2,3},{3,4},{4,5},{5,6},{6,7},{7,0}} | collective-permute-start | bytes 6291464 | tf_op jit(solution)/shard_map/while/body/eval_jaxpr/ppermute | solution.py:30
  98.2 29.2 %collective-permute-start.1 = (bf16[8192,16]{0,1:T(8,128)(2,1)S(1)}, bf16[8192,16]{0,1:T(8,128)(2,1)S(1)}, u32[]{:S(2)}, u32[]{:S(2)}) collective-permute-start(bf16[8192,16]{0,1:T(8,128)(2,1)S(1)} %get-tuple-element.350), channel_id=1, source_target_pairs={{0,1},{1,2},{2,3},{3,4},{4,5},{5,6},{6,7},{7,0}} | collective-permute-start | bytes 786440 | tf_op jit(solution)/shard_map/while/body/eval_jaxpr/ppermute | solution.py:31
  137.8 29.2 %collective-permute-start = (bf16[8192,128]{1,0:T(8,128)(2,1)}, bf16[8192,128]{1,0:T(8,128)(2,1)S(1)}, u32[]{:S(2)}, u32[]{:S(2)}) collective-permute-start(bf16[8192,128]{1,0:T(8,128)(2,1)} %get-tuple-element.349), channel_id=1, source_target_pairs={{0,1},{1,2},{2,3},{3,4},{4,5},{5,6},{6,7},{7,0}} | collective-permute-start | bytes 6291464 | tf_op jit(solution)/shard_map/while/body/eval_jaxpr/ppermute | solution.py:30
  137.8 29.2 %collective-permute-start.1 = (bf16[8192,16]{0,1:T(8,128)(2,1)S(1)}, bf16[8192,16]{0,1:T(8,128)(2,1)S(1)}, u32[]{:S(2)}, u32[]{:S(2)}) collective-permute-start(bf16[8192,16]{0,1:T(8,128)(2,1)S(1)} %get-tuple-element.350), channel_id=1, source_target_pairs={{0,1},{1,2},{2,3},{3,4},{4,5},{5,6},{6,7},{7,0}} | collective-permute-start | bytes 786440 | tf_op jit(solution)/shard_map/while/body/eval_jaxpr/ppermute | solution.py:31
  177.5 29.2 %collective-permute-start = (bf16[8192,128]{1,0:T(8,128)(2,1)}, bf16[8192,128]{1,0:T(8,128)(2,1)S(1)}, u32[]{:S(2)}, u32[]{:S(2)}) collective-permute-start(bf16[8192,128]{1,0:T(8,128)(2,1)} %get-tuple-element.349), channel_id=1, source_target_pairs={{0,1},{1,2},{2,3},{3,4},{4,5},{5,6},{6,7},{7,0}} | collective-permute-start | bytes 6291464 | tf_op jit(solution)/shard_map/while/body/eval_jaxpr/ppermute | solution.py:30
  177.5 29.2 %collective-permute-start.1 = (bf16[8192,16]{0,1:T(8,128)(2,1)S(1)}, bf16[8192,16]{0,1:T(8,128)(2,1)S(1)}, u32[]{:S(2)}, u32[]{:S(2)}) collective-permute-start(bf16[8192,16]{0,1:T(8,128)(2,1)S(1)} %get-tuple-element.350), channel_id=1, source_target_pairs={{0,1},{1,2},{2,3},{3,4},{4,5},{5,6},{6,7},{7,0}} | collective-permute-start | bytes 786440 | tf_op jit(solution)/shard_map/while/body/eval_jaxpr/ppermute | solution.py:31
  217.1 29.2 %collective-permute-start = (bf16[8192,128]{1,0:T(8,128)(2,1)}, bf16[8192,128]{1,0:T(8,128)(2,1)S(1)}, u32[]{:S(2)}, u32[]{:S(2)}) collective-permute-start(bf16[8192,128]{1,0:T(8,128)(2,1)} %get-tuple-element.349), channel_id=1, source_target_pairs={{0,1},{1,2},{2,3},{3,4},{4,5},{5,6},{6,7},{7,0}} | collective-permute-start | bytes 6291464 | tf_op jit(solution)/shard_map/while/body/eval_jaxpr/ppermute | solution.py:30
  217.1 29.2 %collective-permute-start.1 = (bf16[8192,16]{0,1:T(8,128)(2,1)S(1)}, bf16[8192,16]{0,1:T(8,128)(2,1)S(1)}, u32[]{:S(2)}, u32[]{:S(2)}) collective-permute-start(bf16[8192,16]{0,1:T(8,128)(2,1)S(1)} %get-tuple-element.350), channel_id=1, source_target_pairs={{0,1},{1,2},{2,3},{3,4},{4,5},{5,6},{6,7},{7,0}} | collective-permute-start | bytes 786440 | tf_op jit(solution)/shard_map/while/body/eval_jaxpr/ppermute | solution.py:31
  256.7 29.2 %collective-permute-start = (bf16[8192,128]{1,0:T(8,128)(2,1)}, bf16[8192,128]{1,0:T(8,128)(2,1)S(1)}, u32[]{:S(2)}, u32[]{:S(2)}) collective-permute-start(bf16[8192,128]{1,0:T(8,128)(2,1)} %get-tuple-element.349), channel_id=1, source_target_pairs={{0,1},{1,2},{2,3},{3,4},{4,5},{5,6},{6,7},{7,0}} | collective-permute-start | bytes 6291464 | tf_op jit(solution)/shard_map/while/body/eval_jaxpr/ppermute | solution.py:30
  256.8 29.2 %collective-permute-start.1 = (bf16[8192,16]{0,1:T(8,128)(2,1)S(1)}, bf16[8192,16]{0,1:T(8,128)(2,1)S(1)}, u32[]{:S(2)}, u32[]{:S(2)}) collective-permute-start(bf16[8192,16]{0,1:T(8,128)(2,1)S(1)} %get-tuple-element.350), channel_id=1, source_target_pairs={{0,1},{1,2},{2,3},{3,4},{4,5},{5,6},{6,7},{7,0}} | collective-permute-start | bytes 786440 | tf_op jit(solution)/shard_map/while/body/eval_jaxpr/ppermute | solution.py:31
  296.4 0.6 copy-start.2
where the time goes:
time: 297 us
  waiting for transfers between devices  195 us (66%)
  matrix products  64.2 us (22%)
  local copies, waits for them, and re-layouts  19 us (6%)
  other arithmetic  11 us (4%)
  starting transfers between devices  5.61 us (2%)
    ppermute x7, waiting for transfers between devices, shift_step(): v_cur = lax.ppermute(v_cur, 'sp', shift_pairs)  195 us
    dot_general x8, matrix products, block_product(): return jnp.dot(kern_blk, v_rows, preferred_element_type=jnp.float32)  64.2 us
    dot_general x8, other arithmetic, block_product(): jnp.einsum('nd,nd->n', x_rows, x_rows, preferred_element_type=jnp.float32)  10.8 us
    while x14, local copies, waits for them, and re-layouts  9.59 us
  transfers between devices with their start and end apart: 14, of which 7 were waited for; matrix products, arithmetic and copies ran while one was open for 1% of the time, Pallas kernels for 0%

commit v1 on v0

v1 whole, which is shorter than its diff:
```python
import jax
import jax.numpy as jnp
from jax import lax
from jax.experimental import pallas as pl
from jax.experimental.pallas import tpu as pltpu
from jax.sharding import PartitionSpec as P

F32 = jnp.float32
BF16 = jnp.bfloat16
LOG2E = 1.4426950408889634
TILE = 256
CHUNK = 2048
ZROWS = 144
ORDER = (1, 2, 4, 3, 5, 6, 7)


def limbs(r):
    first = r.astype(BF16).astype(F32)
    rest = jnp.where(jnp.abs(first) < jnp.inf, r - first, 0.0)
    second = rest.astype(BF16).astype(F32)
    return first, second, rest - second


def kernel(ls_ref, os_ref, w_ref, z_hbm, x_hbm, v_hbm, o_ref,
           zin, xs, vs, xaug, zall, ysend, yrecv, own,
           in_sem, zs_sem, zr_sem, ys_sem, yr_sem):
    me = lax.axis_index("sp")
    dp = lax.axis_index("dp")
    my_core, my_x, my_y = me % 2, (me // 2) % 2, me // 4

    def peer(k):
        c = (my_core + k % 2) % 2
        x = (my_x + (k // 2) % 2) % 2
        y = (my_y + k // 4) % 2
        return (y * 2 + x) * 2 + c

    zcopy = pltpu.make_async_copy(z_hbm, zin, in_sem.at[0])
    xcopy = pltpu.make_async_copy(x_hbm, xs, in_sem.at[1])
    vcopy = pltpu.make_async_copy(v_hbm, vs, in_sem.at[2])
    zcopy.start()
    xcopy.start()
    vcopy.start()
    barrier = pltpu.get_barrier_semaphore()
    for k in range(1, 8):
        pl.semaphore_signal(barrier, inc=1, device_id=(dp, peer(k)), device_id_type=pl.DeviceIdType.MESH)

    lv = jnp.full((8, 128), ls_ref[0], F32)
    l2 = lv * lv
    pv = jnp.where(l2 > 2.0**64, 2.0**-64, 1.0)
    l2p = l2 * pv
    cvec = LOG2E / l2p
    lns = l2p * jnp.log(jnp.full((8, 128), os_ref[0], F32))
    c = cvec[0, 0]
    s = os_ref[0].astype(BF16)
    sub = lax.broadcasted_iota(jnp.int32, (16, 128), 0)

    zcopy.wait()
    for q in range(4):
        zt = zin[pl.ds(128 * q, 128), :].astype(F32).T
        nz = jnp.sum(zt * zt, axis=0, keepdims=True)
        r = jnp.broadcast_to(nz, (16, 128)) * (-0.5 * pv[0:1, :]) + lns[0:1, :]
        a, b, d = limbs(r)
        aug = jnp.where(sub < 3, 1.0, jnp.where(sub == 3, a, jnp.where(sub == 4, b, jnp.where(sub == 5, d, 0.0))))
        zall[0, q, 0:128, :] = (zt * pv[0:1, :]).astype(BF16)
        zall[0, q, 128:144, :] = aug.astype(BF16)

    def zsend(k):
        return pltpu.make_async_remote_copy(
            src_ref=zall.at[0], dst_ref=zall.at[k], send_sem=zs_sem.at[k - 1], recv_sem=zr_sem.at[k - 1],
            device_id=(dp, peer(k)), device_id_type=pl.DeviceIdType.MESH)

    def ycopy(k):
        return pltpu.make_async_remote_copy(
            src_ref=ysend.at[k - 1], dst_ref=yrecv.at[k - 1], send_sem=ys_sem.at[k - 1], recv_sem=yr_sem.at[k - 1],
            device_id=(dp, peer(k)), device_id_type=pl.DeviceIdType.MESH)

    n_src = xs.shape[0]
    lane = lax.broadcasted_iota(jnp.int32, (TILE, 128), 1)

    def prep(i, carry):
        r0 = pl.multiple_of(i * TILE, TILE)
        xf = xs[pl.ds(r0, TILE), :].astype(F32)
        nx = jnp.sum(xf * xf, axis=1, keepdims=True)
        r = jnp.broadcast_to(nx, (TILE, 128)) * (-0.5 * pv[0:1, :])
        a, b, d = limbs(r)
        aug = jnp.where(lane == 0, a, jnp.where(lane == 1, b, jnp.where(lane == 2, d, jnp.where(lane < 6, 1.0, 0.0))))
        xaug[pl.ds(r0, TILE), :] = aug.astype(BF16)
        return carry

    zero_rows = jnp.zeros((256 - ZROWS, 512), BF16)

    def segment(slot, r0, r1):
        rhs = jnp.concatenate([zall[slot, q] for q in range(4)], axis=1)
        rhs = jnp.concatenate([rhs, zero_rows], axis=0)

        def chunk(i, acc):
            at = pl.multiple_of(i * CHUNK, CHUNK)
            lhs = jnp.concatenate([xs[pl.ds(at, CHUNK), :], xaug[pl.ds(at, CHUNK), :]], axis=1)
            t = jnp.dot(lhs, rhs, preferred_element_type=F32)
            kern = jnp.minimum(jnp.exp2(t * c).astype(BF16), s)
            return acc + jnp.dot(vs[:, pl.ds(at, CHUNK)], kern, preferred_element_type=F32)

        return lax.fori_loop(r0 // CHUNK, r1 // CHUNK, chunk, jnp.zeros((16, 512), F32))

    half = n_src // 2
    xcopy.wait()
    lax.fori_loop(0, half // TILE, prep, 0)
    pl.semaphore_wait(barrier, 7)
    for k in ORDER:
        zsend(k).start()
    lax.fori_loop(half // TILE, n_src // TILE, prep, 0)
    vcopy.wait()
    own[...] = segment(0, 0, half)

    def one(i, table):
        k = table % 8
        zsend(k).wait_recv()
        ysend[k - 1] = segment(k, 0, n_src)
        ycopy(k).start()
        return table // 8

    lax.fori_loop(0, 7, one, sum(k * 8**i for i, k in enumerate(ORDER)))
    own[...] += segment(0, half, n_src)
    total = own[...] * w_ref[0, me].astype(F32)
    for k in ORDER:
        ycopy(k).wait_recv()
        total = total + yrecv[k - 1] * w_ref[0, peer(k)].astype(F32)
    o_ref[...] = total
    for k in ORDER:
        zsend(k).wait_send()
        ycopy(k).wait_send()


def solution(mesh):
    row_spec = P(("dp", "sp"), None)

    def local_fn(z_rows, x_rows, v_rows, mask_row, length_scale, out_scale):
        n_src, r_cols = v_rows.shape
        n_tgt, depth = z_rows.shape
        smem = pl.BlockSpec(memory_space=pltpu.SMEM)
        anywhere = pl.BlockSpec(memory_space=pl.ANY)
        y_t = pl.pallas_call(
            kernel,
            out_shape=jax.ShapeDtypeStruct((r_cols, n_tgt), F32),
            in_specs=[smem, smem, smem, anywhere, anywhere, anywhere],
            out_specs=pl.BlockSpec(memory_space=pltpu.VMEM),
            scratch_shapes=[
                pltpu.VMEM((n_tgt, depth), BF16),
                pltpu.VMEM((n_src, depth), BF16),
                pltpu.VMEM((r_cols, n_src), BF16),
                pltpu.VMEM((n_src, 128), BF16),
                pltpu.VMEM((8, 4, ZROWS, 128), BF16),
                pltpu.VMEM((7, r_cols, n_tgt), F32),
                pltpu.VMEM((7, r_cols, n_tgt), F32),
                pltpu.VMEM((r_cols, n_tgt), F32),
                pltpu.SemaphoreType.DMA((3,)),
                pltpu.SemaphoreType.DMA((7,)),
                pltpu.SemaphoreType.DMA((7,)),
                pltpu.SemaphoreType.DMA((7,)),
                pltpu.SemaphoreType.DMA((7,)),
            ],
            compiler_params=pltpu.CompilerParams(
                collective_id=0, has_side_effects=True, vmem_limit_bytes=40 * 2**20),
        )(length_scale, out_scale, mask_row, z_rows, x_rows, v_rows.T)
        return y_t.T

    return jax.shard_map(local_fn, mesh=mesh, in_specs=(row_spec, row_spec, row_spec, row_spec, P(None), P(None)),
                         out_specs=row_spec, check_vma=False)
```

time: 297 us -> 45.9 us (0.15)
  waiting for transfers between devices: 195 us -> 0 us
  matrix products: 64.2 us -> 0 us
  Pallas kernels: 0 us -> 39.7 us
  local copies, waits for them, and re-layouts: 19 us -> 4.71 us
  other arithmetic: 11 us -> 0 us
  starting transfers between devices: 5.61 us -> 0 us
    ppermute x14 -> x0, waiting for transfers between devices: 195 us -> none  [the longest x7 195 us: shift_step(): v_cur = lax.ppermute(v_cur, 'sp', shift_pairs)]
    dot_general x8 -> x0, matrix products: 64.2 us -> none  [block_product(): return jnp.dot(kern_blk, v_rows, preferred_element_type=jnp.float32)]
    pallas_call x0 -> x1, Pallas kernels: none -> 39.7 us  [local_fn(): pl.pallas_call(kernel, out_shape=jax.ShapeDtypeStruct((r_cols, n_tgt), F3...]
    dot_general x9 -> x0, other arithmetic: 11 us -> none  [the longest x8 10.8 us: block_product(): jnp.einsum('nd,nd->n', x_rows, x_rows, preferred_element_type=jnp.float32)]
    while x14 -> x0, local copies, waits for them, and re-layouts: 9.59 us -> none
    ppermute x14 -> x0, starting transfers between devices: 5.61 us -> none  [the longest x7 4.65 us: shift_step(): v_cur = lax.ppermute(v_cur, 'sp', shift_pairs)]
    dynamic_slice x8 -> x0, local copies, waits for them, and re-layouts: 4.71 us -> none  [the longest x7 4.15 us: shift_step(): return (x_cur, v_cur, y_acc + part_y * weights[src_block])]
  transfers between devices with their start and end apart: 14 -> 0, of which waited for: 7 -> 0; matrix products, arithmetic and copies ran while one was open for 1% -> 0% of each run, Pallas kernels for 0% -> 0%
where the time goes in v1:
time: 45.9 us; the launch traced here: 45.7 us
  Pallas kernels  39.7 us (86%)
  local copies, waits for them, and re-layouts  4.71 us (10%)
  between operations  1.32 us (3%)
    pallas_call x1, Pallas kernels, local_fn(): pl.pallas_call(kernel, out_shape=jax.ShapeDtypeStruct((r_cols, n_tgt), F3...  39.7 us
    unnamed x9, local copies, waits for them, and re-layouts  4.71 us

profile of v1, /device:TPU:0, one launch (start us, length us, event | category | flops | bytes accessed | tf_op | source)
XLA Modules:
  0.0 45.7 jit_solution(14336379678933323654)
XLA Ops:
  1.3 0.0 copy-start
  1.3 1.6 %copy-done = bf16[8192,128]{1,0:T(8,128)(2,1)S(1)} copy-done((bf16[8192,128]{1,0:T(8,128)(2,1)S(1)}, bf16[8192,128]{1,0:T(8,128)(2,1)}, u32[]{:S(2)}) %copy-start) | copy-done | bytes 2097176
  2.9 0.0 copy-start.1
  2.9 0.9 %copy-done.1 = bf16[8192,16]{0,1:T(8,128)(2,1)S(1)} copy-done((bf16[8192,16]{0,1:T(8,128)(2,1)S(1)}, bf16[8192,16]{0,1:T(8,128)(2,1)}, u32[]{:S(2)}) %copy-start.1) | copy-done | bytes 262168
  3.8 0.0 copy-start.2
  3.8 0.9 %copy-done.2 = bf16[512,128]{1,0:T(8,128)(2,1)S(1)} copy-done((bf16[512,128]{1,0:T(8,128)(2,1)S(1)}, bf16[512,128]{1,0:T(8,128)(2,1)}, u32[]{:S(2)}) %copy-start.2) | copy-done | bytes 131096
  4.7 0.0 copy-start.3
  4.7 0.7 %copy-done.3 = s32[1,8]{1,0:T(1,128)S(1)} copy-done((s32[1,8]{1,0:T(1,128)S(1)}, s32[1,8]{1,0:T(1,128)}, u32[]{:S(2)}) %copy-start.3) | copy-done | bytes 56
  5.4 39.7 %shard_map.64 = f32[16,512]{1,0:T(8,128)S(1)} custom-call(f32[1]{0:T(128)S(6)} %copy.8.ls_ref, f32[1]{0:T(128)S(6)} %copy.9.os_ref, s32[1,8]{1,0:T(1,128)S(1)} %copy-done.3, bf16[512,128]{1,0:T(8,128)(2,1)S(1)} %copy-done.2, bf16[8192,128]{1,0:T(8,128)(2,1)S(1)} %copy-done, bf16[16,8192]{1,0:T(8,128)(2,1)S(1)} %bitcast.2), custom_call_target="tpu_custom_call" | custom-call | tf_op jit(solution)/shard_map/pallas_call | solution.py:142
  45.1 0.6 %copy.10 = f32[512,16]{0,1:T(8,128)} copy(f32[512,16]{0,1:T(8,128)S(1)} %bitcast.3) | data formatting | bytes 65536
Async XLA Ops:
  1.3 1.6 %copy-start = (bf16[8192,128]{1,0:T(8,128)(2,1)S(1)}, bf16[8192,128]{1,0:T(8,128)(2,1)}, u32[]{:S(2)}) copy-start(bf16[8192,128]{1,0:T(8,128)(2,1)} %x_hbm.1) | copy-start | bytes 6291460
  2.9 0.9 %copy-start.1 = (bf16[8192,16]{0,1:T(8,128)(2,1)S(1)}, bf16[8192,16]{0,1:T(8,128)(2,1)}, u32[]{:S(2)}) copy-start(bf16[8192,16]{0,1:T(8,128)(2,1)} %param.8) | copy-start | bytes 786436
  3.8 0.9 %copy-start.2 = (bf16[512,128]{1,0:T(8,128)(2,1)S(1)}, bf16[512,128]{1,0:T(8,128)(2,1)}, u32[]{:S(2)}) copy-start(bf16[512,128]{1,0:T(8,128)(2,1)} %z_hbm.1) | copy-start | bytes 393220
  4.7 0.7 %copy-start.3 = (s32[1,8]{1,0:T(1,128)S(1)}, s32[1,8]{1,0:T(1,128)}, u32[]{:S(2)}) copy-start(s32[1,8]{1,0:T(1,128)} %w_ref.1) | copy-start | bytes 100

commit v2 on v1

--- a/solution.py
+++ b/solution.py
@@ -9,7 +9,7 @@
 BF16 = jnp.bfloat16
 LOG2E = 1.4426950408889634
 TILE = 256
-CHUNK = 2048
+CHUNK = 4096
 ZROWS = 144
 ORDER = (1, 2, 4, 3, 5, 6, 7)
 
@@ -21,8 +21,8 @@
     return first, second, rest - second
 
 
-def kernel(ls_ref, os_ref, w_ref, z_hbm, x_hbm, v_hbm, o_ref,
-           zin, xs, vs, xaug, zall, ysend, yrecv, own,
+def kernel(ls_ref, os_ref, w_hbm, z_hbm, x_hbm, v_hbm, o_ref,
+           w_ref, zin, xs, vs, xaug, zall, ysend, yrecv, own,
            in_sem, zs_sem, zr_sem, ys_sem, yr_sem):
     me = lax.axis_index("sp")
     dp = lax.axis_index("dp")
@@ -37,9 +37,11 @@
     zcopy = pltpu.make_async_copy(z_hbm, zin, in_sem.at[0])
     xcopy = pltpu.make_async_copy(x_hbm, xs, in_sem.at[1])
     vcopy = pltpu.make_async_copy(v_hbm, vs, in_sem.at[2])
+    wcopy = pltpu.make_async_copy(w_hbm, w_ref, in_sem.at[3])
     zcopy.start()
     xcopy.start()
     vcopy.start()
+    wcopy.start()
     barrier = pltpu.get_barrier_semaphore()
     for k in range(1, 8):
         pl.semaphore_signal(barrier, inc=1, device_id=(dp, peer(k)), device_id_type=pl.DeviceIdType.MESH)
@@ -87,20 +89,15 @@
         xaug[pl.ds(r0, TILE), :] = aug.astype(BF16)
         return carry
 
-    zero_rows = jnp.zeros((256 - ZROWS, 512), BF16)
-
     def segment(slot, r0, r1):
         rhs = jnp.concatenate([zall[slot, q] for q in range(4)], axis=1)
-        rhs = jnp.concatenate([rhs, zero_rows], axis=0)
-
-        def chunk(i, acc):
-            at = pl.multiple_of(i * CHUNK, CHUNK)
-            lhs = jnp.concatenate([xs[pl.ds(at, CHUNK), :], xaug[pl.ds(at, CHUNK), :]], axis=1)
+        acc = jnp.zeros((16, 512), F32)
+        for at in range(r0, r1, CHUNK):
+            lhs = jnp.concatenate([xs[at:at + CHUNK, :], xaug[at:at + CHUNK, :]], axis=1)[:, :ZROWS]
             t = jnp.dot(lhs, rhs, preferred_element_type=F32)
             kern = jnp.minimum(jnp.exp2(t * c).astype(BF16), s)
-            return acc + jnp.dot(vs[:, pl.ds(at, CHUNK)], kern, preferred_element_type=F32)
-
-        return lax.fori_loop(r0 // CHUNK, r1 // CHUNK, chunk, jnp.zeros((16, 512), F32))
+            acc = acc + jnp.dot(vs[:, at:at + CHUNK], kern, preferred_element_type=F32)
+        return acc
 
     half = n_src // 2
     xcopy.wait()
@@ -121,6 +118,7 @@
 
     lax.fori_loop(0, 7, one, sum(k * 8**i for i, k in enumerate(ORDER)))
     own[...] += segment(0, half, n_src)
+    wcopy.wait()
     total = own[...] * w_ref[0, me].astype(F32)
     for k in ORDER:
         ycopy(k).wait_recv()
@@ -138,13 +136,14 @@
         n_src, r_cols = v_rows.shape
         n_tgt, depth = z_rows.shape
         smem = pl.BlockSpec(memory_space=pltpu.SMEM)
-        anywhere = pl.BlockSpec(memory_space=pl.ANY)
+        anywhere = pl.BlockSpec(memory_space=pltpu.HBM)
         y_t = pl.pallas_call(
             kernel,
             out_shape=jax.ShapeDtypeStruct((r_cols, n_tgt), F32),
-            in_specs=[smem, smem, smem, anywhere, anywhere, anywhere],
+            in_specs=[smem, smem, anywhere, anywhere, anywhere, anywhere],
             out_specs=pl.BlockSpec(memory_space=pltpu.VMEM),
             scratch_shapes=[
+                pltpu.SMEM(mask_row.shape, jnp.int32),
                 pltpu.VMEM((n_tgt, depth), BF16),
                 pltpu.VMEM((n_src, depth), BF16),
                 pltpu.VMEM((r_cols, n_src), BF16),
@@ -153,14 +152,14 @@
                 pltpu.VMEM((7, r_cols, n_tgt), F32),
                 pltpu.VMEM((7, r_cols, n_tgt), F32),
                 pltpu.VMEM((r_cols, n_tgt), F32),
-                pltpu.SemaphoreType.DMA((3,)),
+                pltpu.SemaphoreType.DMA((4,)),
                 pltpu.SemaphoreType.DMA((7,)),
                 pltpu.SemaphoreType.DMA((7,)),
                 pltpu.SemaphoreType.DMA((7,)),
                 pltpu.SemaphoreType.DMA((7,)),
             ],
             compiler_params=pltpu.CompilerParams(
-                collective_id=0, has_side_effects=True, vmem_limit_bytes=40 * 2**20),
+                collective_id=0, has_side_effects=True, vmem_limit_bytes=60 * 2**20),
         )(length_scale, out_scale, mask_row, z_rows, x_rows, v_rows.T)
         return y_t.T
 

time: 45.9 us -> 40.8 us (0.89)
  local copies, waits for them, and re-layouts: 4.71 us -> 1.38 us
  Pallas kernels: 39.7 us -> 37.9 us
    unnamed x9 -> x1, local copies, waits for them, and re-layouts: 4.71 us -> 1.38 us
    pallas_call x1, Pallas kernels: 39.7 us -> 37.9 us  [local_fn(): pl.pallas_call(kernel, out_shape=jax.ShapeDtypeStruct((r_cols, n_tgt), F3...]
where the time goes in v2:
time: 40.8 us; the launch traced here: 40.6 us
  Pallas kernels  37.9 us (93%)
  local copies, waits for them, and re-layouts  1.38 us (3%)
  between operations  1.3 us (3%)
    pallas_call x1, Pallas kernels, local_fn(): pl.pallas_call(kernel, out_shape=jax.ShapeDtypeStruct((r_cols, n_tgt), F3...  37.9 us
    unnamed x1, local copies, waits for them, and re-layouts  1.38 us

profile of v2, /device:TPU:0, one launch (start us, length us, event | category | flops | bytes accessed | tf_op | source)
XLA Modules:
  0.0 40.6 jit_solution(16790038227721242350)
XLA Ops:
  1.3 37.9 %shard_map.64 = f32[16,512]{1,0:T(8,128)} custom-call(f32[1]{0:T(128)S(6)} %copy.8.ls_ref, f32[1]{0:T(128)S(6)} %copy.9.os_ref, s32[1,8]{1,0:T(1,128)} %w_hbm.1, bf16[512,128]{1,0:T(8,128)(2,1)} %z_hbm.1, bf16[8192,128]{1,0:T(8,128)(2,1)} %x_hbm.1, bf16[16,8192]{1,0:T(8,128)(2,1)} %bitcast.2), custom_call_target="tpu_custom_call" | custom-call | tf_op jit(solution)/shard_map/pallas_call | solution.py:140
  39.2 1.4 %copy.10 = f32[512,16]{0,1:T(8,128)} copy(f32[512,16]{0,1:T(8,128)} %bitcast.3) | data formatting | bytes 65536
